TPU v7x, 32 devices: a whole 2x2x4 slice. The times are simulated.
32 devices in a mesh: exp: 4 (over z), hid: 8 (over y, x, core).
Axes of the slice: x: 2, y: 2, z: 4, core: 2. Of those that a mesh axis runs over, the one named last changes fastest.
Arguments:
- tokens: bfloat16 [4, 1024, 1152], P('exp', 'hid'), may hold values from -6 to 6
- route: int32 [4, 1024, 1], P('exp', 'hid'), may hold values from 0 to 3; in each aligned block of 128 rows (0 to 127, 128 to 255, ..., all dimensions but the last counted through in order) at most 40 rows name the same one
- seq_ids: int32 [4, 1024], P('exp', 'hid'), may hold values from 0 to 1, as said below
- cotangent: bfloat16 [4, 1024, 1152], P('exp', 'hid'), may hold values from -6 to 6
- gain_one: bfloat16 [1152], replicated, may hold values from 0.5 to 1.5
- gain_two: bfloat16 [1152], replicated, may hold values from 0.5 to 1.5
- in_weight: bfloat16 [1152, 4608], P(None, ('exp', 'hid')), may hold values from -0.1875 to 0.1875
- conv_weight: bfloat16 [4, 2304], P(None, ('exp', 'hid')), may hold values from -3 to 3
- conv_bias: bfloat16 [2304], P(('exp', 'hid')), may hold values from -0.5 to 0.5
- x_weight: bfloat16 [2304, 104], P(('exp', 'hid')), may hold values from -0.125 to 0.125
- dt_weight: bfloat16 [72, 2304], P(None, ('exp', 'hid')), may hold values from -0.75 to 0.75
- dt_bias: bfloat16 [2304], P(('exp', 'hid')), may hold values from -6 to -2
- a_log: bfloat16 [2304, 16], P(('exp', 'hid')), may hold values from -6 to 2.75
- skip: bfloat16 [2304], P(('exp', 'hid')), may hold values from 0.5 to 1.5
- out_weight: bfloat16 [2304, 1152], P(('exp', 'hid')), may hold values from -0.125 to 0.125
- expert_in: bfloat16 [4, 1152, 3072], P('exp', None, 'hid'), may hold values from -0.1875 to 0.1875
- expert_out: bfloat16 [4, 3072, 1152], P('exp', 'hid'), may hold values from -0.109375 to 0.109375
Outputs:
- output: bfloat16 [4, 1024, 1152], P('exp', 'hid')
- grad_tokens: float32 [4, 1024, 1152], P('exp', 'hid')
- grad_gain_one: float32 [1152], replicated
- grad_gain_two: float32 [1152], replicated
- grad_in_weight: float32 [1152, 4608], P(None, ('exp', 'hid'))
- grad_conv_weight: float32 [4, 2304], P(None, ('exp', 'hid'))
- grad_conv_bias: float32 [2304], P(('exp', 'hid'))
- grad_x_weight: float32 [2304, 104], P(('exp', 'hid'))
- grad_dt_weight: float32 [72, 2304], P(None, ('exp', 'hid'))
- grad_dt_bias: float32 [2304], P(('exp', 'hid'))
- grad_a_log: float32 [2304, 16], P(('exp', 'hid'))
- grad_skip: float32 [2304], P(('exp', 'hid'))
- grad_out_weight: float32 [2304, 1152], P(('exp', 'hid'))
- grad_expert_in: float32 [4, 1152, 3072], P('exp', None, 'hid')
- grad_expert_out: float32 [4, 3072, 1152], P('exp', 'hid')
Inputs may be any that keep to these rules, and one draw needn't show every extreme that they name: `route`: the rows of one device name no expert more than 40 times; in every draw some expert is named exactly 40 times by the rows of some device. `seq_ids`: each packed row holds one or two sequences: ids start at 0 and rise by one at most once; the first row is one whole sequence; in every other row the second sequence starts at position 256 or later.
All inputs are finite; a program needn't handle non-finite values.
Results may differ from a plain program's by a relative error of at most 0.014.
Values may be sent and summed in bfloat16 or wider, within the bound.
A program may use at most 384 MiB of HBM per device.

v0:
```python
import jax
import jax.numpy as jnp
from jax import lax
from jax.sharding import PartitionSpec as P

EPSILON = 1e-05
ROOT_HALF = 0.7071067811865476
INV_ROOT_TWO_PI = 0.3989422804014327


def passed_along(value, axis, steps):
    count = lax.axis_size(axis)
    leading, last = (max(0, -steps), min(count, count - steps))
    return lax.ppermute(value, axis, [(source, source + steps) for source in range(leading, last)])


def entering(value, axis, join, neutral, backward):
    count, mine = (lax.axis_size(axis), lax.axis_index(axis))
    pieces = jax.tree.map(lambda part: lax.all_gather(part, axis), value)
    if backward:
        pieces = jax.tree.map(lambda part: part[::-1], pieces)
        mine = count - 1 - mine
    running = jax.tree.map(
        lambda part, zero: jnp.full_like(part, 0) + jnp.asarray(zero, part.dtype), value, neutral
    )

    def lap(position, running):
        longer = join(running, jax.tree.map(lambda part: part[position], pieces))
        return jax.tree.map(lambda new, old: jnp.where(position < mine, new, old), longer, running)

    return lax.fori_loop(0, count - 1, lap, running)


def rms_scale(values, gain_vec):
    inverse = lax.rsqrt(jnp.mean(values * values, axis=-1, keepdims=True) + EPSILON)
    return values * inverse * gain_vec


def gelu_slope(values):
    cumulative = 0.5 * (1.0 + jax.scipy.special.erf(values * ROOT_HALF))
    return cumulative + values * INV_ROOT_TWO_PI * jnp.exp(-0.5 * values * values)


def silu_slope(values):
    sigmoid_of = jax.nn.sigmoid(values)
    return sigmoid_of + values * sigmoid_of * (1.0 - sigmoid_of)


def chain_combine(earlier, latter):
    return (earlier[0] * latter[0], latter[0] * earlier[1] + latter[1])


def mat_nn(left_side, right_side):
    return jnp.dot(left_side, right_side, preferred_element_type=jnp.float32)


def mat_tn(left_side, right_side):
    return lax.dot_general(
        left_side, right_side, (((0,), (0,)), ((), ())), preferred_element_type=jnp.float32
    )


def mat_nt(left_side, right_side):
    return lax.dot_general(
        left_side, right_side, (((1,), (1,)), ((), ())), preferred_element_type=jnp.float32
    )


def doubling(decays, drives):
    length = decays.shape[0]
    offset = 1
    while offset < length:
        prev_decay = jnp.concatenate(
            [jnp.ones_like(decays[:offset]), decays[: length - offset]], axis=0
        )
        prev_drive = jnp.concatenate(
            [jnp.zeros_like(drives[:offset]), drives[: length - offset]], axis=0
        )
        drives = decays * prev_drive + drives
        decays = decays * prev_decay
        offset = offset * 2
    return (drives, decays)


def per_device(
    tokens,
    route,
    seq_ids,
    cotangent,
    gain_one,
    gain_two,
    in_weight,
    conv_weight,
    conv_bias,
    x_weight,
    dt_weight,
    dt_bias,
    a_log,
    skip,
    out_weight,
    expert_in,
    expert_out,
):
    gathered = (
        lax.all_gather(in_weight, ("exp", "hid"), axis=1, tiled=True),
        lax.all_gather(conv_weight, ("exp", "hid"), axis=1, tiled=True),
        lax.all_gather(conv_bias, ("exp", "hid"), axis=0, tiled=True),
        lax.all_gather(x_weight, ("exp", "hid"), axis=0, tiled=True),
        lax.all_gather(dt_weight, ("exp", "hid"), axis=1, tiled=True),
        lax.all_gather(dt_bias, ("exp", "hid"), axis=0, tiled=True),
        lax.all_gather(a_log, ("exp", "hid"), axis=0, tiled=True),
        lax.all_gather(skip, ("exp", "hid"), axis=0, tiled=True),
        lax.all_gather(out_weight, ("exp", "hid"), axis=0, tiled=True),
    )
    w_in, w_conv, b_conv, w_x, w_dt, b_dt, w_alog, w_skip, w_out = gathered
    row_count = tokens.shape[1]
    model_width = tokens.shape[2]
    inner_width = w_x.shape[0]
    state_width = w_alog.shape[1]
    rank_width = w_dt.shape[0]
    conv_taps = w_conv.shape[0]
    rim_rows = conv_taps - 1
    x_rows = tokens[0].astype(jnp.float32)
    seq_float = seq_ids[0].astype(jnp.float32)
    gain_first = gain_one.astype(jnp.float32)
    gain_second = gain_two.astype(jnp.float32)
    tap_values = w_conv.astype(jnp.float32)
    conv_shift = b_conv.astype(jnp.float32)
    step_bias = b_dt.astype(jnp.float32)
    skip_gain = w_skip.astype(jnp.float32)
    a_trans = -jnp.exp(jnp.transpose(w_alog.astype(jnp.float32)))
    unit_state = jnp.ones((state_width, inner_width), jnp.float32)
    zero_state = jnp.zeros_like(unit_state)
    normed_one = rms_scale(x_rows, gain_first)
    normed_low = normed_one.astype(jnp.bfloat16)
    proj_both = mat_nn(normed_low, w_in)
    conv_in = proj_both[:, :inner_width]
    gate_in = proj_both[:, inner_width:]
    prev_rows, prev_seq = passed_along(
        (conv_in[row_count - rim_rows :], seq_float[row_count - rim_rows :]), "hid", 1
    )
    ext_rows = jnp.concatenate([prev_rows, conv_in], axis=0)
    ext_seq = jnp.concatenate([prev_seq, seq_float], axis=0)
    matches = [
        (ext_seq[k : k + row_count] == seq_float).astype(jnp.float32) for k in range(conv_taps)
    ]
    conv_out = conv_shift[None] + jnp.zeros_like(conv_in)
    for k in range(conv_taps):
        conv_out = (
            conv_out + tap_values[k][None] * matches[k][:, None] * ext_rows[k : k + row_count]
        )
    activated = jax.nn.silu(conv_out)
    act_low = activated.astype(jnp.bfloat16)
    x_double = mat_nn(act_low, w_x)
    dt_low = x_double[:, :rank_width].astype(jnp.bfloat16)
    b_proj = x_double[:, rank_width : rank_width + state_width]
    c_proj = x_double[:, rank_width + state_width :]
    pre_step = mat_nn(dt_low, w_dt) + step_bias[None]
    step_size = jax.nn.softplus(pre_step)
    carries_on = matches[conv_taps - 2]
    drive_in = step_size * activated
    decays = jnp.exp(step_size[:, None, :] * a_trans[None]) * carries_on[:, None, None]
    drives = b_proj[:, :, None] * drive_in[:, None, :]
    local_states, products = doubling(decays, drives)
    _, incoming = entering(
        (products[-1], local_states[-1]), "hid", chain_combine, (unit_state, zero_state), False
    )
    states = local_states + products * incoming[None]
    state_out = jnp.sum(states * c_proj[:, :, None], axis=1) + skip_gain[None] * activated
    gate_silu = jax.nn.silu(gate_in)
    mixed_low = (state_out * gate_silu).astype(jnp.bfloat16)
    hidden_one = x_rows + mat_nn(mixed_low, w_out)
    normed_two = rms_scale(hidden_one, gain_second)
    two_low = normed_two.astype(jnp.bfloat16)
    back_low = cotangent[0]
    expert_count = lax.axis_size("exp")
    capacity = 5 * row_count // (4 * expert_count)
    slot_count = expert_count * capacity
    chosen = route[0, :, 0]
    picks = (chosen[:, None] == jnp.arange(expert_count, dtype=jnp.int32)[None]).astype(jnp.int32)
    ranks = jnp.cumsum(picks, axis=0) - 1
    slot_of = jnp.sum(picks * ranks, axis=1)
    place = (
        (chosen * capacity + slot_of)[:, None] == jnp.arange(slot_count, dtype=jnp.int32)[None]
    ).astype(jnp.bfloat16)
    send_rows = (
        mat_tn(place, two_low).astype(jnp.bfloat16).reshape(expert_count, capacity, model_width)
    )
    send_grads = (
        mat_tn(place, back_low).astype(jnp.bfloat16).reshape(expert_count, capacity, model_width)
    )
    got_rows, got_grads = (
        lax.all_to_all(send_rows, "exp", split_axis=0, concat_axis=0, tiled=True),
        lax.all_to_all(send_grads, "exp", split_axis=0, concat_axis=0, tiled=True),
    )
    got_rows = got_rows.reshape(slot_count, model_width)
    got_grads = got_grads.reshape(slot_count, model_width)
    first_slice = expert_in[0]
    second_slice = expert_out[0]
    rows_piece = lax.all_gather(got_rows, "hid", axis=0, tiled=True)
    grads_piece = lax.all_gather(got_grads, "hid", axis=0, tiled=True)
    pre_act = mat_nn(rows_piece, first_slice)
    hidden_piece = jax.nn.gelu(pre_act, approximate=False).astype(jnp.bfloat16)
    grad_piece = (mat_nt(grads_piece, second_slice) * gelu_slope(pre_act)).astype(jnp.bfloat16)
    first_acc = mat_tn(rows_piece, grad_piece)
    second_acc = mat_tn(hidden_piece, grads_piece)
    grad_first = first_acc[None]
    grad_second = second_acc[None]
    summed = lax.psum_scatter(
        jnp.concatenate(
            [mat_nn(hidden_piece, second_slice), mat_nt(grad_piece, first_slice)], axis=1
        ),
        "hid",
        scatter_dimension=0,
        tiled=True,
    )
    out_slots = (
        summed[:, :model_width].astype(jnp.bfloat16).reshape(expert_count, capacity, model_width)
    )
    grad_slots = (
        summed[:, model_width:].astype(jnp.bfloat16).reshape(expert_count, capacity, model_width)
    )
    ret_out, ret_grad = (
        lax.all_to_all(out_slots, "exp", split_axis=0, concat_axis=0, tiled=True),
        lax.all_to_all(grad_slots, "exp", split_axis=0, concat_axis=0, tiled=True),
    )
    branch_two = mat_nn(place, ret_out.reshape(slot_count, model_width))
    grad_normed = mat_nn(place, ret_grad.reshape(slot_count, model_width))
    result = (hidden_one + branch_two).astype(jnp.bfloat16)[None]
    _, norm_two_pull = jax.vjp(rms_scale, hidden_one, gain_second)
    grad_h_norm, grad_gain_second = norm_two_pull(grad_normed)
    grad_hidden = back_low.astype(jnp.float32) + grad_h_norm
    grad_mix = grad_hidden.astype(jnp.bfloat16)
    grad_out_w = mat_tn(mixed_low, grad_mix)
    grad_mixed = mat_nt(grad_mix, w_out)
    grad_state_out = grad_mixed * gate_silu
    grad_gate = grad_mixed * state_out * silu_slope(gate_in)
    grad_skip = jnp.sum(grad_state_out * activated, axis=0)
    grad_act = grad_state_out * skip_gain[None]
    direct = c_proj[:, :, None] * grad_state_out[:, None, :]
    flip_sends, flip_products = doubling(jnp.flip(decays, 0), jnp.flip(decays * direct, 0))
    _, later_adjoint = entering(
        (products[-1], flip_sends[-1]), "hid", chain_combine, (unit_state, zero_state), True
    )
    sends = jnp.flip(flip_sends + flip_products * later_adjoint[None], 0)
    adjoint = direct + jnp.concatenate([sends[1:], later_adjoint[None]], axis=0)
    before = jnp.concatenate([incoming[None], states[:-1]], axis=0)
    pulled = adjoint * before * decays
    grad_b = jnp.sum(adjoint * drive_in[:, None, :], axis=2)
    grad_drive = jnp.sum(adjoint * b_proj[:, :, None], axis=1)
    grad_c = jnp.sum(states * grad_state_out[:, None, :], axis=2)
    grad_amat = jnp.sum(pulled * step_size[:, None, :], axis=0)
    grad_step = jnp.sum(pulled * a_trans[None], axis=1) + grad_drive * activated
    grad_act = grad_act + grad_drive * step_size
    grad_pre_step = (grad_step * jax.nn.sigmoid(pre_step)).astype(jnp.bfloat16)
    grad_dt_bias = jnp.sum(grad_pre_step.astype(jnp.float32), axis=0)
    grad_dt_w = mat_tn(dt_low, grad_pre_step)
    grad_rank = mat_nt(grad_pre_step, w_dt)
    grad_double = jnp.concatenate([grad_rank, grad_b, grad_c], axis=1).astype(jnp.bfloat16)
    grad_x_w = mat_tn(act_low, grad_double)
    grad_act = grad_act + mat_nt(grad_double, w_x)
    grad_conv = grad_act * silu_slope(conv_out)
    next_grad, next_seq = passed_along((grad_conv[:rim_rows], seq_float[:rim_rows]), "hid", -1)
    ext_grad = jnp.concatenate([grad_conv, next_grad], axis=0)
    ext_seq_after = jnp.concatenate([seq_float, next_seq], axis=0)
    grad_conv_in = jnp.zeros_like(grad_conv)
    tap_grads = []
    for k in range(conv_taps):
        tap_grads.append(
            jnp.sum(grad_conv * matches[k][:, None] * ext_rows[k : k + row_count], axis=0)
        )
        agree_after = (ext_seq_after[rim_rows - k : rim_rows - k + row_count] == seq_float).astype(
            jnp.float32
        )
        grad_conv_in = (
            grad_conv_in
            + tap_values[k][None]
            * agree_after[:, None]
            * ext_grad[rim_rows - k : rim_rows - k + row_count]
        )
    grad_conv_w = jnp.stack(tap_grads, axis=0)
    grad_conv_b = jnp.sum(grad_conv, axis=0)
    grad_proj = jnp.concatenate([grad_conv_in, grad_gate], axis=1).astype(jnp.bfloat16)
    grad_in_w = mat_tn(normed_low, grad_proj)
    grad_normed_one = mat_nt(grad_proj, w_in)
    _, norm_one_pull = jax.vjp(rms_scale, x_rows, gain_first)
    grad_x_norm, grad_gain_first = norm_one_pull(grad_normed_one)
    grad_tokens = (grad_hidden + grad_x_norm)[None]
    grad_alog = jnp.transpose(grad_amat * a_trans)
    mamba_sums = (
        lax.psum_scatter(grad_in_w, ("exp", "hid"), scatter_dimension=1, tiled=True),
        lax.psum_scatter(grad_conv_w, ("exp", "hid"), scatter_dimension=1, tiled=True),
        lax.psum_scatter(grad_conv_b, ("exp", "hid"), scatter_dimension=0, tiled=True),
        lax.psum_scatter(grad_x_w, ("exp", "hid"), scatter_dimension=0, tiled=True),
        lax.psum_scatter(grad_dt_w, ("exp", "hid"), scatter_dimension=1, tiled=True),
        lax.psum_scatter(grad_dt_bias, ("exp", "hid"), scatter_dimension=0, tiled=True),
        lax.psum_scatter(grad_alog, ("exp", "hid"), scatter_dimension=0, tiled=True),
        lax.psum_scatter(grad_skip, ("exp", "hid"), scatter_dimension=0, tiled=True),
        lax.psum_scatter(grad_out_w, ("exp", "hid"), scatter_dimension=0, tiled=True),
    )
    gain_sums = lax.psum((grad_gain_first, grad_gain_second), ("exp", "hid"))
    return (
        result,
        grad_tokens,
        gain_sums[0],
        gain_sums[1],
        mamba_sums[0],
        mamba_sums[1],
        mamba_sums[2],
        mamba_sums[3],
        mamba_sums[4],
        mamba_sums[5],
        mamba_sums[6],
        mamba_sums[7],
        mamba_sums[8],
        grad_first,
        grad_second,
    )


def solution(mesh):
    return jax.shard_map(
        per_device,
        mesh=mesh,
        in_specs=(
            P("exp", "hid", None),
            P("exp", "hid", None),
            P("exp", "hid"),
            P("exp", "hid", None),
            P(),
            P(),
            P(None, ("exp", "hid")),
            P(None, ("exp", "hid")),
            P(("exp", "hid")),
            P(("exp", "hid"), None),
            P(None, ("exp", "hid")),
            P(("exp", "hid")),
            P(("exp", "hid"), None),
            P(("exp", "hid")),
            P(("exp", "hid"), None),
            P("exp", None, "hid"),
            P("exp", "hid", None),
        ),
        out_specs=(
            P("exp", "hid", None),
            P("exp", "hid", None),
            P(),
            P(),
            P(None, ("exp", "hid")),
            P(None, ("exp", "hid")),
            P(("exp", "hid")),
            P(("exp", "hid"), None),
            P(None, ("exp", "hid")),
            P(("exp", "hid")),
            P(("exp", "hid"), None),
            P(("exp", "hid")),
            P(("exp", "hid"), None),
            P("exp", None, "hid"),
            P("exp", "hid", None),
        ),
        check_vma=False,
    )
```

profile of v0, /device:TPU:0, one launch (start us, length us, event | category | flops | bytes accessed | tf_op | source)
XLA Modules:
  0.0 2271.7 jit_solution(12910804265100206754)
XLA Ops:
  15.7 45.5 %all-reduce.41 = (bf16[2304]{0:T(1024)(128)(2,1)S(1)}, bf16[2304]{0:T(1024)(128)(2,1)S(1)}, bf16[2304]{0:T(1024)(128)(2,1)}) all-reduce(bf16[2304]{0:T(1024)(128)(2,1)S(1)} %dynamic-update-slice.1, bf16[2304]{0:T(1024)(128)(2,1)S(1)} %dynamic-update-slice, ...), channel_id=1, replica_groups=mesh['exp'=4,'hid'=8] {'exp','hid'}, use_global_device_ids=true, to_apply=%add.29 | all-reduce | flops 6912 | bytes 27648
  61.1 42.6 %all-gather = bf16[32,72,4]{1,2,0:T(4,128)(2,1)S(1)} all-gather(bf16[1,72,4]{1,2,0:T(4,128)(2,1)} %bitcast.143), channel_id=1, replica_groups=mesh['exp'=4,'hid'=8] {'exp','hid'}, dimensions={0}, use_global_device_ids=true | all-gather | bytes 19008 | tf_op jit(solution)/shard_map/all_gather | solution.py:106
  104.7 37.2 %all-gather.1 = bf16[32,72,16]{1,2,0:T(8,128)(2,1)S(1)} all-gather(bf16[1,72,16]{1,2,0:T(8,128)(2,1)} %bitcast.140), channel_id=1, replica_groups=mesh['exp'=4,'hid'=8] {'exp','hid'}, dimensions={0}, use_global_device_ids=true | all-gather | bytes 76032 | tf_op jit(solution)/shard_map/all_gather | solution.py:111
  142.6 39.7 %all_gather.47 = bf16[72,2304]{0,1:T(8,128)(2,1)S(1)} all-gather(bf16[72,72]{0,1:T(8,128)(2,1)S(1)} %copy.57), channel_id=1, replica_groups=mesh['exp'=4,'hid'=8] {'exp','hid'}, dimensions={1}, use_global_device_ids=true | all-gather | bytes 342144 | tf_op jit(solution)/shard_map/all_gather | solution.py:109
  182.3 38.2 %all_gather.46 = bf16[2304,104]{1,0:T(8,128)(2,1)S(1)} all-gather(bf16[72,104]{1,0:T(8,128)(2,1)S(1)} %copy-done.82), channel_id=1, replica_groups=mesh['exp'=4,'hid'=8] {'exp','hid'}, dimensions={0}, use_global_device_ids=true | all-gather | bytes 494208 | tf_op jit(solution)/shard_map/all_gather | solution.py:108
  304.6 32.8 %multiply_add_fusion.13 = (f32[128,16,2304]{2,1,0:T(8,128)}, f32[128,16,2304]{2,1,0:T(8,128)}) fusion(f32[128,16,2304]{2,1,0:T(8,128)} %get-tuple-element.328, f32[126,16,2304]{2,1,0:T(8,128)} %slice.291, f32[127,16,2304]{2,1,0:T(8,128)} %get-tuple-element.325, f32[128]{0:T(128)S(1)} %get-tuple-element.343, f32[16,2304]{1,0:T(8,128)S(1)} %bitcast.129, ...), kind=kLoop, calls=%fused_computation.36 | loop fusion | flops 23592960 | bytes 95257088 | tf_op jit(solution)/shard_map/add | solution.py:79
  362.0 37.7 %multiply_add_fusion.12 = (f32[128,16,2304]{2,1,0:T(8,128)}, f32[128,16,2304]{2,1,0:T(8,128)}) fusion(f32[128,16,2304]{2,1,0:T(8,128)} %get-tuple-element.321, f32[124,16,2304]{2,1,0:T(8,128)} %slice.292, f32[128,16,2304]{2,1,0:T(8,128)} %get-tuple-element.322, f32[126,16,2304]{2,1,0:T(8,128)} %slice.284), kind=kLoop, calls=%fused_computation.35 | loop fusion | flops 14155776 | bytes 112361472 | tf_op jit(solution)/shard_map/add | solution.py:79
  424.0 37.6 %multiply_add_fusion.11 = (f32[128,16,2304]{2,1,0:T(8,128)}, f32[128,16,2304]{2,1,0:T(8,128)}) fusion(f32[128,16,2304]{2,1,0:T(8,128)} %get-tuple-element.319, f32[120,16,2304]{2,1,0:T(8,128)} %slice.293, f32[128,16,2304]{2,1,0:T(8,128)} %get-tuple-element.320, f32[124,16,2304]{2,1,0:T(8,128)} %slice.285), kind=kLoop, calls=%fused_computation.34 | loop fusion | flops 14155776 | bytes 111476736 | tf_op jit(solution)/shard_map/add | solution.py:79
  485.3 37.0 %multiply_add_fusion.10 = (f32[128,16,2304]{2,1,0:T(8,128)}, f32[128,16,2304]{2,1,0:T(8,128)}) fusion(f32[128,16,2304]{2,1,0:T(8,128)} %get-tuple-element.317, f32[112,16,2304]{2,1,0:T(8,128)} %slice.294, f32[128,16,2304]{2,1,0:T(8,128)} %get-tuple-element.318, f32[120,16,2304]{2,1,0:T(8,128)} %slice.286), kind=kLoop, calls=%fused_computation.33 | loop fusion | flops 14155776 | bytes 109707264 | tf_op jit(solution)/shard_map/add | solution.py:79
  544.8 36.1 %multiply_add_fusion.9 = (f32[128,16,2304]{2,1,0:T(8,128)}, f32[128,16,2304]{2,1,0:T(8,128)}) fusion(f32[128,16,2304]{2,1,0:T(8,128)} %get-tuple-element.315, f32[96,16,2304]{2,1,0:T(8,128)} %slice.295, f32[128,16,2304]{2,1,0:T(8,128)} %get-tuple-element.316, f32[112,16,2304]{2,1,0:T(8,128)} %slice.287), kind=kLoop, calls=%fused_computation.32 | loop fusion | flops 14155776 | bytes 106168320 | tf_op jit(solution)/shard_map/add | solution.py:79
  596.3 31.7 %multiply_add_fusion.8 = (f32[128,16,2304]{2,1,0:T(8,128)}, f32[128,16,2304]{2,1,0:T(8,128)}) fusion(f32[128,16,2304]{2,1,0:T(8,128)} %get-tuple-element.313, f32[64,16,2304]{2,1,0:T(8,128)S(1)} %slice.296, f32[128,16,2304]{2,1,0:T(8,128)} %get-tuple-element.314, f32[96,16,2304]{2,1,0:T(8,128)} %slice.288), kind=kLoop, calls=%fused_computation.31 | loop fusion | flops 14155776 | bytes 99090432 | tf_op jit(solution)/shard_map/add | solution.py:79
  733.0 33.4 %all-gather.16.cloned.1.call-done = bf16[2304,1152]{1,0:T(8,128)(2,1)} async-done(((bf16[72,1152]{1,0:T(8,128)(2,1)}), bf16[2304,1152]{1,0:T(8,128)(2,1)}) %all-gather.16.cloned.1.call-update) | async-done | bytes 5308432 | tf_op jit(solution)/shard_map/all_gather | solution.py:113
  884.6 88.5 %reduce-scatter.16.cloned.1.call-done = f32[160,2304]{1,0:T(8,128)} async-done(((f32[1280,2304]{1,0:T(8,128)}), f32[160,2304]{1,0:T(8,128)}) %reduce-scatter.16.cloned.1.call-update) | async-done | bytes 1474576 | tf_op jit(solution)/shard_map/reduce_scatter | solution.py:209
  1062.2 37.9 %multiply_add_fusion.6 = (f32[128,16,2304]{2,1,0:T(8,128)}, f32[128,16,2304]{2,1,0:T(8,128)}) fusion(f32[128,16,2304]{2,1,0:T(8,128)} %copy-done.4, f32[126,16,2304]{2,1,0:T(8,128)} %slice.311, f32[127,16,2304]{2,1,0:T(8,128)} %slice.247, f32[128,16,2304]{2,1,0:T(8,128)} %copy-done.2), kind=kLoop, calls=%fused_computation.20 | loop fusion | flops 14155776 | bytes 112803840 | tf_op jit(solution)/shard_map/add | solution.py:79
  1124.8 37.8 %multiply_add_fusion.5 = (f32[128,16,2304]{2,1,0:T(8,128)}, f32[128,16,2304]{2,1,0:T(8,128)}) fusion(f32[128,16,2304]{2,1,0:T(8,128)} %get-tuple-element.307, f32[124,16,2304]{2,1,0:T(8,128)} %slice.312, f32[128,16,2304]{2,1,0:T(8,128)} %get-tuple-element.308, f32[126,16,2304]{2,1,0:T(8,128)} %slice.305), kind=kLoop, calls=%fused_computation.19 | loop fusion | flops 14155776 | bytes 112361472 | tf_op jit(solution)/shard_map/add | solution.py:79
  1187.0 37.6 %multiply_add_fusion.4 = (f32[128,16,2304]{2,1,0:T(8,128)}, f32[128,16,2304]{2,1,0:T(8,128)}) fusion(f32[128,16,2304]{2,1,0:T(8,128)} %get-tuple-element.305, f32[120,16,2304]{2,1,0:T(8,128)} %slice.313, f32[128,16,2304]{2,1,0:T(8,128)} %get-tuple-element.306, f32[124,16,2304]{2,1,0:T(8,128)} %slice.306), kind=kLoop, calls=%fused_computation.18 | loop fusion | flops 14155776 | bytes 111476736 | tf_op jit(solution)/shard_map/add | solution.py:79
  1248.1 37.3 %multiply_add_fusion.3 = (f32[128,16,2304]{2,1,0:T(8,128)}, f32[128,16,2304]{2,1,0:T(8,128)}) fusion(f32[128,16,2304]{2,1,0:T(8,128)} %get-tuple-element.303, f32[112,16,2304]{2,1,0:T(8,128)} %slice.314, f32[128,16,2304]{2,1,0:T(8,128)} %get-tuple-element.304, f32[120,16,2304]{2,1,0:T(8,128)} %slice.307), kind=kLoop, calls=%fused_computation.17 | loop fusion | flops 14155776 | bytes 109707264 | tf_op jit(solution)/shard_map/add | solution.py:79
  1307.7 36.1 %multiply_add_fusion.2 = (f32[128,16,2304]{2,1,0:T(8,128)}, f32[128,16,2304]{2,1,0:T(8,128)}) fusion(f32[128,16,2304]{2,1,0:T(8,128)} %get-tuple-element.301, f32[96,16,2304]{2,1,0:T(8,128)} %slice.315, f32[128,16,2304]{2,1,0:T(8,128)} %get-tuple-element.302, f32[112,16,2304]{2,1,0:T(8,128)} %slice.308), kind=kLoop, calls=%fused_computation.16 | loop fusion | flops 14155776 | bytes 106168320 | tf_op jit(solution)/shard_map/add | solution.py:79
  1359.0 31.7 %multiply_add_fusion.1 = (f32[128,16,2304]{2,1,0:T(8,128)}, f32[128,16,2304]{2,1,0:T(8,128)}) fusion(f32[128,16,2304]{2,1,0:T(8,128)} %get-tuple-element.299, f32[64,16,2304]{2,1,0:T(8,128)S(1)} %slice.316, f32[128,16,2304]{2,1,0:T(8,128)} %get-tuple-element.300, f32[96,16,2304]{2,1,0:T(8,128)} %slice.309), kind=kLoop, calls=%fused_computation.15 | loop fusion | flops 14155776 | bytes 99090432 | tf_op jit(solution)/shard_map/add | solution.py:79
  1555.7 93.0 %all-reduce.45.cloned.1.call-done = (f32[1152]{0:T(1024)}, f32[1152]{0:T(1024)}, f32[4,2304]{1,0:T(4,128)}, f32[2304]{0:T(1024)}, f32[2304]{0:T(1024)}, /*index=5*/f32[2304]{0:T(1024)}) async-done(((f32[1152]{0:T(1024)}, f32[1152]{0:T(1024)}, f32[4,2304]{1,0:T(4,128)}, f32[2304]{0:T(1024)}, f32[2304]{0:T(1024)}, /*index=5*/f32[2304]{0:T(1024)}), (f32[1152]{0:T(1024)}, f32[1152]{0:T(1024)}, ...) | async-done | bytes 73744 | tf_op jit(solution)/shard_map/psum | solution.py:301
  1653.9 130.8 %all-reduce.47.cloned.1.call-done = (f32[72,2304]{1,0:T(8,128)}, f32[2304,16]{0,1:T(8,128)}) async-done(((f32[72,2304]{1,0:T(8,128)}, f32[2304,16]{0,1:T(8,128)}), (f32[72,2304]{1,0:T(8,128)}, f32[2304,16]{0,1:T(8,128)})) %all-reduce.47.cloned.1.call-update) | async-done | bytes 811024
  1787.7 100.1 %reduce-scatter.18.cloned.1.call-done = f32[72,104]{1,0:T(8,128)} async-done(((f32[2304,104]{1,0:T(8,128)}), f32[72,104]{1,0:T(8,128)}) %reduce-scatter.18.cloned.1.call-update) | async-done | bytes 29968
  1887.8 147.8 %reduce-scatter.20.cloned.1.call-done = f32[72,1152]{1,0:T(8,128)} async-done(((f32[2304,1152]{1,0:T(8,128)}), f32[72,1152]{1,0:T(8,128)}) %reduce-scatter.20.cloned.1.call-update) | async-done | bytes 331792
  2035.6 226.5 %reduce-scatter.14.cloned.1.call-done = f32[1152,144]{0,1:T(8,128)} async-done(((f32[1152,4608]{0,1:T(8,128)}), f32[1152,144]{0,1:T(8,128)}) %reduce-scatter.14.cloned.1.call-update) | async-done | bytes 663568 | tf_op jit(solution)/shard_map/reduce_scatter | solution.py:291
  (413 shorter events, 809.2 us)
Async XLA Ops:
  7.2 807.7 %copy-start = (bf16[1,1152,384]{2,1,0:T(8,128)(2,1)S(1)}, bf16[1,1152,384]{2,1,0:T(8,128)(2,1)}, u32[]{:S(2)}) copy-start(bf16[1,1152,384]{2,1,0:T(8,128)(2,1)} %param.36) | copy-start | bytes 2654212
  7.2 213.5 %all-gather.10.cloned.1.call-start = ((), (), s32[]{:S(2)}) async-start(), calls=%async_computation.8 | async-start | bytes 10948608 | tf_op jit(solution)/shard_map/all_gather | solution.py:105
  8.0 663.6 %all-gather.12.cloned.1.call-start = ((), (), s32[]{:S(2)}) async-start(), calls=%async_computation.9 | async-start | bytes 1327104 | tf_op jit(solution)/shard_map/all_gather | solution.py:19
  8.7 211.9 %collective-permute-start = (f32[3]{0:T(128)S(1)}, f32[3]{0:T(128)S(1)}, u32[]{:S(2)}, u32[]{:S(2)}) collective-permute-start(f32[3]{0:T(128)S(1)} %get-tuple-element.348), channel_id=1, source_target_pairs={{0,1},{1,2},{2,3},{3,4},{4,5},{5,6},{6,7},{8,9},{9,10},{10,11},{11... | collective-permute-start | bytes 44 | tf_op jit(solution)/shard_map/ppermute | solution.py:14
  11.1 209.5 %collective-permute-start.2 = (f32[3]{0:T(128)S(1)}, f32[3]{0:T(128)S(1)}, u32[]{:S(2)}, u32[]{:S(2)}) collective-permute-start(f32[3]{0:T(128)S(1)} %get-tuple-element.347), channel_id=1, source_target_pairs={{1,0},{2,1},{3,2},{4,3},{5,4},{6,5},{7,6},{9,8},{10,9},{11,10},{12... | collective-permute-start | bytes 44 | tf_op jit(solution)/shard_map/ppermute | solution.py:14
  13.1 215.2 %copy-start.64 = (f32[1152]{0:T(1024)}, f32[1152]{0:T(1024)S(1)}, u32[]{:S(2)}) copy-start(f32[1152]{0:T(1024)S(1)} %convert_element_type.118) | copy-start | bytes 13828
  228.3 3.1 collective-permute-start.1
  647.9 50.1 %all-gather.14.cloned.1.call-start = ((), (), s32[]{:S(2)}) async-start(), calls=%async_computation.10 | async-start | bytes 1327104 | tf_op jit(solution)/shard_map/all_gather | solution.py:19
  649.5 116.9 %all-gather.16.cloned.1.call-start = ((), (), s32[]{:S(2)}) async-start(), calls=%async_computation.11 | async-start | bytes 5474304 | tf_op jit(solution)/shard_map/all_gather | solution.py:113
  650.1 164.8 %all-gather.18.cloned.1.call-start = ((), (), s32[]{:S(2)}) async-start(), calls=%async_computation.12 | async-start | bytes 3317760 | tf_op jit(solution)/shard_map/all_gather | solution.py:200
  650.7 342.3 %copy-start.88 = (s32[128]{0:T(128)}, s32[128]{0:T(128)S(1)}, u32[]{:S(2)}) copy-start(s32[128]{0:T(128)S(1)} %multiply_add_fusion.17) | copy-start | bytes 1540
  769.9 224.0 %copy-start.15 = (f32[128,1152]{1,0:T(8,128)}, f32[128,1152]{1,0:T(8,128)S(1)}, u32[]{:S(2)}) copy-start(f32[128,1152]{1,0:T(8,128)S(1)} %get-tuple-element.353) | copy-start | bytes 1769476
  785.3 62.8 %all-gather.20.cloned.1.call-start = ((), (), s32[]{:S(2)}) async-start(), calls=%async_computation.13 | async-start | bytes 3317760 | tf_op jit(solution)/shard_map/all_gather | solution.py:201
  799.8 173.3 %reduce-scatter.16.cloned.1.call-start = ((), (), s32[]{:S(2)}) async-start(), calls=%async_computation.16 | async-start | bytes 13271040 | tf_op jit(solution)/shard_map/reduce_scatter | solution.py:209
  975.5 17.5 all-to-all-start.3
  980.1 436.8 %all-gather.22.cloned.1.call-start = ((), (), s32[]{:S(2)}) async-start(), calls=%async_computation.14 | async-start | bytes 1327104 | tf_op jit(solution)/shard_map/all_gather | solution.py:19
  1392.3 256.4 %all-reduce.45.cloned.1.call-start = ((), (), s32[]{:S(2)}) async-start(), calls=%async_computation.19 | async-start | bytes 180224 | tf_op jit(solution)/shard_map/psum | solution.py:301
  1510.9 3.2 collective-permute-start.3
  1518.4 266.2 %all-reduce.47.cloned.1.call-start = ((), (), s32[]{:S(2)}) async-start(), calls=%async_computation.20 | async-start | bytes 1622016
  1519.6 368.1 %reduce-scatter.18.cloned.1.call-start = ((), (), s32[]{:S(2)}) async-start(), calls=%async_computation.17 | async-start | bytes 1216512
  1521.3 514.3 %reduce-scatter.20.cloned.1.call-start = ((), (), s32[]{:S(2)}) async-start(), calls=%async_computation.18 | async-start | bytes 10948608
  1526.9 735.2 %reduce-scatter.14.cloned.1.call-start = ((), (), s32[]{:S(2)}) async-start(), calls=%async_computation.15 | async-start | bytes 21897216 | tf_op jit(solution)/shard_map/reduce_scatter | solution.py:291
  1536.9 16.7 all-to-all-start.2
  1546.7 718.0 %copy-start.1 = (bf16[1,1152,384]{2,1,0:T(8,128)(2,1)S(1)}, bf16[1,1152,384]{2,1,0:T(8,128)(2,1)}, u32[]{:S(2)}) copy-start(bf16[1,1152,384]{2,1,0:T(8,128)(2,1)} %param.36) | copy-start | bytes 2654212
  (104 other events, 2167.8 us)
Sparse Core Ops, SparseCore 0:
  10.9 89.7 all-gather.9
  648.0 23.5 all-gather.11
  674.0 23.9 all-gather.13
  700.8 65.5 all-gather.15
  785.4 29.4 all-gather.17
  816.6 31.3 all-gather.19
  884.7 88.3 reduce-scatter.15
  1392.5 24.3 all-gather.21
  1518.6 130.0 all-reduce.44
  1653.8 130.8 all-reduce.46
  1790.3 97.3 reduce-scatter.17
  1894.3 141.2 reduce-scatter.19
  2042.6 219.4 reduce-scatter.13
where the time goes:
time: 2280 us; the launch traced here: 2270 us
  waiting for transfers between devices  916 us (40%)
  other arithmetic  611 us (27%)
  local copies, waits for them, and re-layouts  398 us (17%)
  blocking collectives  232 us (10%)
  matrix products  80.3 us (4%)
    add x13, other arithmetic, doubling(): drives = decays * prev_drive + drives  450 us
    unnamed x16, waiting for transfers between devices  380 us
    reduce_scatter x1, waiting for transfers between devices, per_device(): lax.psum_scatter(grad_in_w, ('exp', 'hid'), scatter_dimension=1, tiled=True)  226 us
    slice x14, local copies, waits for them, and re-layouts, doubling(): decays[:length - offset]  163 us
    slice x15, local copies, waits for them, and re-layouts, doubling(): drives[:length - offset]  119 us
    psum x1, waiting for transfers between devices, per_device(): gain_sums = lax.psum((grad_gain_first, grad_gain_second), ('exp', 'hid'))  93 us
    reduce_scatter x1, waiting for transfers between devices, per_device(): lax.psum_scatter(jnp.concatenate([mat_nn(hidden_piece, second_slice), mat...  88.5 us
    unnamed x234, local copies, waits for them, and re-layouts  82.6 us
  transfers between devices with their start and end apart: 19, of which 15 were waited for; matrix products, arithmetic and copies ran while one was open for 5% of the time, Pallas kernels for 0%

commit v1 on v0

v1 whole, which is shorter than its diff:
```python
import functools

import jax
import jax.numpy as jnp
from jax import lax
from jax.experimental import pallas as pl
from jax.experimental.pallas import tpu as pltpu
from jax.sharding import PartitionSpec as P

EPSILON = 1e-05
ROOT_HALF = 0.7071067811865476
INV_ROOT_TWO_PI = 0.3989422804014327
LOG2_E = 1.4426950408889634
LN_2 = 0.6931471805599453
CUT_STEP = 1e6
SUB = 16


def rms_scale(values, gain_vec):
    inverse = lax.rsqrt(jnp.mean(values * values, axis=-1, keepdims=True) + EPSILON)
    return values * inverse * gain_vec


def gelu_slope(values):
    cumulative = 0.5 * (1.0 + jax.scipy.special.erf(values * ROOT_HALF))
    return cumulative + values * INV_ROOT_TWO_PI * jnp.exp(-0.5 * values * values)


def silu_slope(values):
    sigmoid_of = jax.nn.sigmoid(values)
    return sigmoid_of + values * sigmoid_of * (1.0 - sigmoid_of)


def mat_nn(left_side, right_side):
    return jnp.dot(left_side, right_side, preferred_element_type=jnp.float32)


def mat_tn(left_side, right_side):
    return lax.dot_general(
        left_side, right_side, (((0,), (0,)), ((), ())), preferred_element_type=jnp.float32
    )


def mat_nt(left_side, right_side):
    return lax.dot_general(
        left_side, right_side, (((1,), (1,)), ((), ())), preferred_element_type=jnp.float32
    )


def group_ones(states):
    rows = lax.broadcasted_iota(jnp.int32, (SUB, SUB * states), 0)
    cols = lax.broadcasted_iota(jnp.int32, (SUB, SUB * states), 1)
    low = rows * states
    return jnp.where((cols >= low) & (cols < low + states), 1.0, 0.0).astype(jnp.bfloat16)


def scan_fwd_kernel(step_ref, drive_ref, bc_ref, a_ref, y_ref, start_ref, state, prod):
    states, _ = a_ref.shape
    block = step_ref.shape[0]

    @pl.when(pl.program_id(0) == 0)
    def _():
        state[...] = jnp.zeros_like(state)

    start_ref[0] = state[...]
    a_val = a_ref[...]

    def sub(k, s):
        base = pl.multiple_of(k * SUB, SUB)
        bc = bc_ref[k]
        for tt in range(SUB):
            row = base + tt
            decay = jnp.exp2(step_ref[pl.ds(row, 1), :] * a_val)
            s = decay * s + bc[:states, tt : tt + 1] * drive_ref[pl.ds(row, 1), :]
            at = pl.multiple_of(row * states, states)
            prod[pl.ds(at, states), :] = (s * bc[states:, tt : tt + 1]).astype(jnp.bfloat16)
        return s

    state[...] = lax.fori_loop(0, block // SUB, sub, state[...])
    ones = group_ones(states)
    for k in range(block // SUB):
        y_ref[k * SUB : (k + 1) * SUB, :] = mat_nn(
            ones, prod[k * SUB * states : (k + 1) * SUB * states, :]
        )


def scan_bwd_kernel(
    step_ref,
    drive_ref,
    grad_ref,
    bc_ref,
    a_ref,
    start_ref,
    gdrive_ref,
    gstep_ref,
    gb_ref,
    gc_ref,
    ga_ref,
    carry,
    decays,
    before,
    prod_b,
    prod_c,
    prod_d,
    prod_s,
):
    states, _ = a_ref.shape
    block = step_ref.shape[0]

    @pl.when(pl.program_id(0) == 0)
    def _():
        carry[...] = jnp.zeros_like(carry)
        ga_ref[...] = jnp.zeros_like(ga_ref)

    a_val = a_ref[...]

    def ahead(k, s):
        base = pl.multiple_of(k * SUB, SUB)
        bc = bc_ref[k]
        for tt in range(SUB):
            row = base + tt
            decay = jnp.exp2(step_ref[pl.ds(row, 1), :] * a_val)
            decays[row] = decay
            before[row] = s
            s = decay * s + bc[:states, tt : tt + 1] * drive_ref[pl.ds(row, 1), :]
            at = pl.multiple_of(row * states, states)
            prod_c[pl.ds(at, states), :] = (s * grad_ref[pl.ds(row, 1), :]).astype(jnp.bfloat16)
        return s

    lax.fori_loop(0, block // SUB, ahead, start_ref[0])

    def back(turn, held):
        q, ga = held
        k = block // SUB - 1 - turn
        base = pl.multiple_of(k * SUB, SUB)
        bc = bc_ref[k]
        for tt in reversed(range(SUB)):
            row = base + tt
            at = pl.multiple_of(row * states, states)
            adjoint = grad_ref[pl.ds(row, 1), :] * bc[states:, tt : tt + 1] + q
            prod_b[pl.ds(at, states), :] = (adjoint * drive_ref[pl.ds(row, 1), :]).astype(
                jnp.bfloat16
            )
            prod_d[pl.ds(at, states), :] = (adjoint * bc[:states, tt : tt + 1]).astype(
                jnp.bfloat16
            )
            q = decays[row] * adjoint
            pulled = q * before[row]
            ga = ga + pulled * step_ref[pl.ds(row, 1), :]
            prod_s[pl.ds(at, states), :] = (pulled * a_val).astype(jnp.bfloat16)
        return q, ga

    q, ga = lax.fori_loop(0, block // SUB, back, (carry[...], ga_ref[...]))
    carry[...] = q
    ga_ref[...] = ga
    ones = group_ones(states)
    lane_ones = jnp.ones((8, a_val.shape[1]), jnp.bfloat16)
    for k in range(block // SUB):
        rows = slice(k * SUB * states, (k + 1) * SUB * states)
        gdrive_ref[k * SUB : (k + 1) * SUB, :] = mat_nn(ones, prod_d[rows, :])
        gstep_ref[k * SUB : (k + 1) * SUB, :] = mat_nn(ones, prod_s[rows, :])
        gb_ref[0, :, rows] = mat_nt(lane_ones, prod_b[rows, :])
        gc_ref[0, :, rows] = mat_nt(lane_ones, prod_c[rows, :])


def scan_forward(step_cut, drive, bc, a_two, block):
    length, width = step_cut.shape
    states = a_two.shape[0]
    turns = length // block
    rows = pl.BlockSpec((block, width), lambda i: (i, 0))
    cost = pl.CostEstimate(
        flops=8 * length * width * states,
        transcendentals=length * width * states,
        bytes_accessed=12 * length * width,
    )
    return pl.pallas_call(
        scan_fwd_kernel,
        grid=(turns,),
        in_specs=[
            rows,
            rows,
            pl.BlockSpec((block // SUB, 2 * states, SUB), lambda i: (i, 0, 0)),
            pl.BlockSpec((states, width), lambda i: (0, 0)),
        ],
        out_specs=[rows, pl.BlockSpec((1, states, width), lambda i: (i, 0, 0))],
        out_shape=[
            jax.ShapeDtypeStruct((length, width), jnp.float32),
            jax.ShapeDtypeStruct((turns, states, width), jnp.float32),
        ],
        scratch_shapes=[
            pltpu.VMEM((states, width), jnp.float32),
            pltpu.VMEM((block * states, width), jnp.bfloat16),
        ],
        cost_estimate=cost,
        name="scan_forward",
    )(step_cut, drive, bc, a_two)


def scan_backward(step_cut, drive, grad, bc, a_two, starts, block):
    length, width = step_cut.shape
    states = a_two.shape[0]
    turns = length // block
    rows = pl.BlockSpec((block, width), lambda i: (turns - 1 - i, 0))
    flat = pl.BlockSpec((1, 8, block * states), lambda i: (turns - 1 - i, 0, 0))
    whole = pl.BlockSpec((states, width), lambda i: (0, 0))
    cost = pl.CostEstimate(
        flops=24 * length * width * states,
        transcendentals=length * width * states,
        bytes_accessed=20 * length * width,
    )
    product = pltpu.VMEM((block * states, width), jnp.bfloat16)
    history = pltpu.VMEM((block, states, width), jnp.float32)
    return pl.pallas_call(
        scan_bwd_kernel,
        grid=(turns,),
        in_specs=[
            rows,
            rows,
            rows,
            pl.BlockSpec((block // SUB, 2 * states, SUB), lambda i: (turns - 1 - i, 0, 0)),
            whole,
            pl.BlockSpec((1, states, width), lambda i: (turns - 1 - i, 0, 0)),
        ],
        out_specs=[rows, rows, flat, flat, whole],
        out_shape=[
            jax.ShapeDtypeStruct((length, width), jnp.float32),
            jax.ShapeDtypeStruct((length, width), jnp.float32),
            jax.ShapeDtypeStruct((turns, 8, block * states), jnp.float32),
            jax.ShapeDtypeStruct((turns, 8, block * states), jnp.float32),
            jax.ShapeDtypeStruct((states, width), jnp.float32),
        ],
        scratch_shapes=[
            pltpu.VMEM((states, width), jnp.float32),
            history,
            history,
            product,
            product,
            product,
            product,
        ],
        cost_estimate=cost,
        name="scan_backward",
    )(step_cut, drive, grad, bc, a_two, starts)


def routing(exp_count, hid_count):
    pairs = []
    for j in range(exp_count * hid_count):
        half, bit = j // 2, j % 2
        pairs.append((j, (2 * (half // hid_count) + bit) * hid_count + half % hid_count))
    return pairs


def per_device(
    tokens,
    route,
    seq_ids,
    cotangent,
    gain_one,
    gain_two,
    in_weight,
    conv_weight,
    conv_bias,
    x_weight,
    dt_weight,
    dt_bias,
    a_log,
    skip,
    out_weight,
    expert_in,
    expert_out,
):
    both = ("exp", "hid")
    exp_count = lax.axis_size("exp")
    hid_count = lax.axis_size("hid")
    row_count = tokens.shape[1]
    model_width = tokens.shape[2]
    own = x_weight.shape[0]
    width = own * exp_count
    length = row_count * hid_count
    rank = dt_weight.shape[0]
    states = a_log.shape[1]
    taps = conv_weight.shape[0]
    pairs = routing(exp_count, hid_count)

    x_rows = tokens[0].astype(jnp.float32)
    gain_first = gain_one.astype(jnp.float32)
    gain_second = gain_two.astype(jnp.float32)
    back_low = cotangent[0]

    small = jnp.concatenate(
        [
            x_weight,
            dt_weight.T,
            a_log,
            conv_weight.T,
            conv_bias[:, None],
            dt_bias[:, None],
            skip[:, None],
        ],
        axis=1,
    )
    small_width = small.shape[1]
    pad = -small_width % 128
    packed = jnp.concatenate(
        [out_weight, small, jnp.zeros((own, pad), jnp.bfloat16)], axis=1
    )
    routed = lax.ppermute(packed, both, pairs)
    w_in = lax.all_gather(in_weight.T, "exp", axis=0, tiled=True)
    w_all = lax.all_gather(routed, "exp", axis=0, tiled=True)
    w_conv_in, w_gate = w_in[:width], w_in[width:]
    w_out = w_all[:, :model_width]
    w_small = w_all[:, model_width:]
    at = 0
    w_x = w_small[:, at : at + rank + 2 * states]
    at += rank + 2 * states
    w_dt = w_small[:, at : at + rank]
    at += rank
    alog_rows = w_small[:, at : at + states]
    at += states
    tap_rows = w_small[:, at : at + taps].astype(jnp.float32).T
    at += taps
    conv_shift = w_small[:, at].astype(jnp.float32)
    step_bias = w_small[:, at + 1].astype(jnp.float32)
    skip_gain = w_small[:, at + 2].astype(jnp.float32)
    a_neg = -jnp.exp(alog_rows.astype(jnp.float32)).T
    a_two = a_neg * LOG2_E

    normed_low = lax.all_gather(
        rms_scale(x_rows, gain_first).astype(jnp.bfloat16), "hid", axis=0, tiled=True
    )
    seq_row = lax.all_gather(seq_ids[0], "hid", axis=0, tiled=True)
    conv_in = mat_nt(normed_low, w_conv_in)
    gate_in = mat_nt(normed_low, w_gate)
    rim = taps - 1
    ext_rows = jnp.concatenate([jnp.zeros((rim, width), jnp.float32), conv_in], axis=0)
    ext_seq = jnp.concatenate([jnp.full((rim,), -1, jnp.int32), seq_row], axis=0)
    matches = [
        (ext_seq[k : k + length] == seq_row).astype(jnp.float32)[:, None] for k in range(taps)
    ]
    conv_out = conv_shift[None] + jnp.zeros_like(conv_in)
    for k in range(taps):
        conv_out = conv_out + tap_rows[k][None] * matches[k] * ext_rows[k : k + length]
    activated = jax.nn.silu(conv_out)
    act_low = activated.astype(jnp.bfloat16)
    x_double = lax.psum(mat_nn(act_low, w_x), "hid")
    dt_low = x_double[:, :rank].astype(jnp.bfloat16)
    bc = x_double[:, rank:].reshape(length // SUB, SUB, 2 * states).transpose(0, 2, 1)
    pre_step = mat_nt(dt_low, w_dt) + step_bias[None]
    step_size = jax.nn.softplus(pre_step)
    step_cut = jnp.where(matches[taps - 2] > 0.5, step_size, CUT_STEP)
    drive = step_size * activated
    scanned, starts = scan_forward(step_cut, drive, bc, a_two, row_count)
    state_out = scanned + skip_gain[None] * activated
    gate_silu = jax.nn.silu(gate_in)
    mixed_low = (state_out * gate_silu).astype(jnp.bfloat16)
    mixed_sum = lax.psum_scatter(
        mat_nn(mixed_low, w_out).astype(jnp.bfloat16), "hid", scatter_dimension=0, tiled=True
    )
    hidden_one = x_rows + mixed_sum.astype(jnp.float32)
    two_low = rms_scale(hidden_one, gain_second).astype(jnp.bfloat16)

    capacity = 5 * row_count // (4 * exp_count)
    slot_count = exp_count * capacity
    chosen = route[0, :, 0]
    picks = (chosen[:, None] == jnp.arange(exp_count, dtype=jnp.int32)[None]).astype(jnp.int32)
    ranks = jnp.cumsum(picks, axis=0) - 1
    slot_of = jnp.sum(picks * ranks, axis=1)
    place = (
        (chosen * capacity + slot_of)[:, None] == jnp.arange(slot_count, dtype=jnp.int32)[None]
    ).astype(jnp.bfloat16)

    def to_expert(rows):
        slots = mat_tn(place, rows).astype(jnp.bfloat16)
        slots = slots.reshape(exp_count, capacity, model_width)
        got = lax.all_to_all(slots, "exp", split_axis=0, concat_axis=0, tiled=True)
        got = got.reshape(slot_count, model_width)
        return lax.all_gather(got, "hid", axis=0, tiled=True)

    grads_piece = to_expert(back_low)
    rows_piece = to_expert(two_low)
    first_slice = expert_in[0]
    second_slice = expert_out[0]
    pre_act = mat_nn(rows_piece, first_slice)
    hidden_piece = jax.nn.gelu(pre_act, approximate=False).astype(jnp.bfloat16)
    grad_piece = (mat_nt(grads_piece, second_slice) * gelu_slope(pre_act)).astype(jnp.bfloat16)
    grad_first = mat_tn(rows_piece, grad_piece)[None]
    grad_second = mat_tn(hidden_piece, grads_piece)[None]
    summed = lax.psum_scatter(
        jnp.concatenate(
            [mat_nn(hidden_piece, second_slice), mat_nt(grad_piece, first_slice)], axis=1
        ).astype(jnp.bfloat16),
        "hid",
        scatter_dimension=0,
        tiled=True,
    )
    returned = lax.all_to_all(
        summed.reshape(exp_count, capacity, 2 * model_width),
        "exp",
        split_axis=0,
        concat_axis=0,
        tiled=True,
    ).reshape(slot_count, 2 * model_width)
    spread = mat_nn(place, returned)
    branch_two = spread[:, :model_width]
    grad_normed = spread[:, model_width:]
    result = (hidden_one + branch_two).astype(jnp.bfloat16)[None]
    _, norm_two_pull = jax.vjp(rms_scale, hidden_one, gain_second)
    grad_h_norm, grad_gain_second = norm_two_pull(grad_normed)
    grad_hidden = back_low.astype(jnp.float32) + grad_h_norm

    grad_mix = lax.all_gather(grad_hidden.astype(jnp.bfloat16), "hid", axis=0, tiled=True)
    grad_out_w = mat_tn(mixed_low, grad_mix)
    grad_mixed = mat_nt(grad_mix, w_out)
    grad_state_out = grad_mixed * gate_silu
    grad_gate = (grad_mixed * state_out * silu_slope(gate_in)).astype(jnp.bfloat16)
    grad_skip = jnp.sum(grad_state_out * activated, axis=0)
    grad_drive, grad_cut, gb_flat, gc_flat, grad_amat = scan_backward(
        step_cut, drive, grad_state_out, bc, a_two, starts, row_count
    )
    grad_b = gb_flat[:, 0, :].reshape(length, states)
    grad_c = gc_flat[:, 0, :].reshape(length, states)
    grad_step = grad_cut * LN_2 + grad_drive * activated
    grad_act = grad_state_out * skip_gain[None] + grad_drive * step_size
    grad_pre_step = (grad_step * jax.nn.sigmoid(pre_step)).astype(jnp.bfloat16)
    grad_dt_bias = jnp.sum(grad_pre_step.astype(jnp.float32), axis=0)
    grad_dt_w = mat_tn(grad_pre_step, dt_low)
    grad_double = lax.psum(
        jnp.concatenate([mat_nn(grad_pre_step, w_dt), grad_b, grad_c], axis=1), "hid"
    ).astype(jnp.bfloat16)
    grad_x_w = mat_tn(act_low, grad_double)
    grad_act = grad_act + mat_nt(grad_double, w_x)
    grad_conv = grad_act * silu_slope(conv_out)
    ext_grad = jnp.concatenate([grad_conv, jnp.zeros((rim, width), jnp.float32)], axis=0)
    ext_after = jnp.concatenate([seq_row, jnp.full((rim,), -1, jnp.int32)], axis=0)
    grad_conv_in = jnp.zeros_like(grad_conv)
    tap_grads = []
    for k in range(taps):
        tap_grads.append(jnp.sum(grad_conv * matches[k] * ext_rows[k : k + length], axis=0))
        agree = (ext_after[rim - k : rim - k + length] == seq_row).astype(jnp.float32)[:, None]
        grad_conv_in = (
            grad_conv_in + tap_rows[k][None] * agree * ext_grad[rim - k : rim - k + length]
        )
    grad_conv_b = jnp.sum(grad_conv, axis=0)
    grad_conv_low = grad_conv_in.astype(jnp.bfloat16)
    grad_in_conv = mat_tn(grad_conv_low, normed_low)
    grad_in_gate = mat_tn(grad_gate, normed_low)
    grad_normed_one = lax.psum_scatter(
        (mat_nn(grad_conv_low, w_conv_in) + mat_nn(grad_gate, w_gate)).astype(jnp.bfloat16),
        "hid",
        scatter_dimension=0,
        tiled=True,
    ).astype(jnp.float32)
    _, norm_one_pull = jax.vjp(rms_scale, x_rows, gain_first)
    grad_x_norm, grad_gain_first = norm_one_pull(grad_normed_one)
    grad_tokens = (grad_hidden + grad_x_norm)[None]

    grad_small = jnp.concatenate(
        [
            grad_x_w,
            grad_dt_w,
            (grad_amat * a_neg).T,
            jnp.stack(tap_grads + [grad_conv_b, grad_dt_bias, grad_skip], axis=1),
            jnp.zeros((width, pad), jnp.float32),
        ],
        axis=1,
    )
    backs = [(target, source) for source, target in pairs]
    in_sum = lax.psum_scatter(
        jnp.concatenate([grad_in_conv, grad_in_gate], axis=0).astype(jnp.bfloat16),
        "exp",
        scatter_dimension=0,
        tiled=True,
    ).astype(jnp.float32)
    rest_sum = lax.psum_scatter(
        jnp.concatenate([grad_out_w, grad_small], axis=1), "exp", scatter_dimension=0, tiled=True
    )
    rest_own = lax.ppermute(rest_sum, both, backs)
    small_own = rest_own[:, model_width:]
    at = rank + 2 * states
    at_alog = at + rank
    at_taps = at_alog + states
    at_bias = at_taps + taps
    gain_sums = lax.psum((grad_gain_first, grad_gain_second), both)
    return (
        result,
        grad_tokens,
        gain_sums[0],
        gain_sums[1],
        in_sum.T,
        small_own[:, at_taps:at_bias].T,
        small_own[:, at_bias],
        small_own[:, :at],
        small_own[:, at:at_alog].T,
        small_own[:, at_bias + 1],
        small_own[:, at_alog:at_taps],
        small_own[:, at_bias + 2],
        rest_own[:, :model_width],
        grad_first,
        grad_second,
    )


def solution(mesh):
    flat = ("exp", "hid")
    return jax.shard_map(
        per_device,
        mesh=mesh,
        in_specs=(
            P("exp", "hid", None),
            P("exp", "hid", None),
            P("exp", "hid"),
            P("exp", "hid", None),
            P(),
            P(),
            P(None, flat),
            P(None, flat),
            P(flat),
            P(flat, None),
            P(None, flat),
            P(flat),
            P(flat, None),
            P(flat),
            P(flat, None),
            P("exp", None, "hid"),
            P("exp", "hid", None),
        ),
        out_specs=(
            P("exp", "hid", None),
            P("exp", "hid", None),
            P(),
            P(),
            P(None, flat),
            P(None, flat),
            P(flat),
            P(flat, None),
            P(None, flat),
            P(flat),
            P(flat, None),
            P(flat),
            P(flat, None),
            P("exp", None, "hid"),
            P("exp", "hid", None),
        ),
        check_vma=False,
    )
```

time: 2280 us -> 719 us (0.32)
  waiting for transfers between devices: 916 us -> 330 us
  other arithmetic: 611 us -> 25.1 us
  local copies, waits for them, and re-layouts: 398 us -> 42.9 us
  blocking collectives: 232 us -> 165 us
  Pallas kernels: 0 us -> 52.4 us
    add x16 -> x1, other arithmetic: 474 us -> 1.19 us  [per_device(): conv_out + tap_rows[k][None] * matches[k] * ext_rows[k:k + length]]
    unnamed x16 -> x12, waiting for transfers between devices: 380 us -> 36.3 us
    slice x43 -> x9, local copies, waits for them, and re-layouts: 314 us -> 8.71 us  [the longest x1 1.72 us: per_device(): rest_own[:, :model_width]]
    reduce_scatter x1 -> x3, waiting for transfers between devices: 226 us -> 84.9 us  [the longest x1 41.6 us: per_device(): lax.psum_scatter(mat_nn(mixed_low, w_out).astype(jnp.bfloat16), 'hid', sc...]
    all_gather x4 -> x2, blocking collectives: 158 us -> 44.4 us  [the longest x1 31.4 us: per_device(): w_all = lax.all_gather(routed, 'exp', axis=0, tiled=True)]
    psum x0 -> x2, blocking collectives: none -> 67.7 us  [the longest x1 39.5 us: per_device(): gain_sums = lax.psum((grad_gain_first, grad_gain_second), both)]
    reduce_sum x3, other arithmetic: 71.5 us -> 3.85 us  [the longest x1 2.43 us: per_device(): jnp.sum(grad_conv * matches[k] * ext_rows[k:k + length], axis=0)]
    unnamed x234 -> x104, local copies, waits for them, and re-layouts: 82.6 us -> 15.8 us
  transfers between devices with their start and end apart: 19 -> 13, of which waited for: 15 -> 10; matrix products, arithmetic and copies ran while one was open for 5% -> 7% of each run, Pallas kernels for 0% -> 0%
where the time goes in v1:
time: 719 us; the launch traced here: 710 us
  waiting for transfers between devices  330 us (46%)
  blocking collectives  165 us (23%)
  matrix products  73.3 us (10%)
  Pallas kernels  52.4 us (7%)
  local copies, waits for them, and re-layouts  42.9 us (6%)
  other arithmetic  25.1 us (3%)
  between operations  15 us (2%)
    reduce_scatter x1, waiting for transfers between devices, per_device(): lax.psum_scatter(jnp.concatenate([mat_nn(hidden_piece, second_slice), mat...  59.7 us
    psum x1, waiting for transfers between devices, per_device(): x_double = lax.psum(mat_nn(act_low, w_x), 'hid')  53.3 us
    reduce_scatter x1, waiting for transfers between devices, per_device(): lax.psum_scatter(mat_nn(mixed_low, w_out).astype(jnp.bfloat16), 'hid', sc...  41.6 us
    reduce_scatter x1, waiting for transfers between devices, per_device(): lax.psum_scatter((mat_nn(grad_conv_low, w_conv_in) + mat_nn(grad_gate, w_...  39.8 us
    psum x1, blocking collectives, per_device(): gain_sums = lax.psum((grad_gain_first, grad_gain_second), both)  39.5 us
    all_gather x2, waiting for transfers between devices, to_expert(): return lax.all_gather(got, 'hid', axis=0, tiled=True)  39.3 us
    pallas_call x1, Pallas kernels, scan_backward(): pl.pallas_call(scan_bwd_kernel, grid=(turns,), in_specs=[rows, rows, rows...  37.3 us
    unnamed x12, waiting for transfers between devices  36.3 us
  transfers between devices with their start and end apart: 13, of which 10 were waited for; matrix products, arithmetic and copies ran while one was open for 7% of the time, Pallas kernels for 0%

profile of v1, /device:TPU:0, one launch (start us, length us, event | category | flops | bytes accessed | tf_op | source)
XLA Modules:
  0.0 709.9 jit_solution(12340231451281354830)
XLA Ops:
  14.7 12.9 %all-gather = s32[1,1024]{1,0:T(1,128)S(1)} all-gather(s32[1,128]{1,0:T(1,128)S(1)} %copy-done.42), channel_id=2, replica_groups=mesh['exp'=4,'hid'=8] {'hid'}, dimensions={1}, use_global_device_ids=true | all-gather | bytes 4608 | tf_op jit(solution)/shard_map/all_gather | solution.py:332
  27.7 31.4 %all_gather.22 = bf16[288,1408]{1,0:T(8,128)(2,1)S(1)} all-gather(bf16[72,1408]{1,0:T(8,128)(2,1)S(1)} %collective-permute-done), channel_id=1, replica_groups=mesh['exp'=4,'hid'=8] {'exp'}, dimensions={0}, use_global_device_ids=true | all-gather | bytes 1013760 | tf_op jit(solution)/shard_map/all_gather | solution.py:310
  60.1 29.7 %all-gather.7.cloned.1.call-done = bf16[1024,1152]{1,0:T(8,128)(2,1)} async-done(((bf16[128,1152]{1,0:T(8,128)(2,1)}), bf16[1024,1152]{1,0:T(8,128)(2,1)}) %all-gather.7.cloned.1.call-update) | async-done | bytes 2359312 | tf_op jit(solution)/shard_map/all_gather | solution.py:329
  98.4 53.3 %all-reduce.9.cloned.1.call-done = f32[1024,104]{0,1:T(8,128)} async-done(((f32[1024,104]{0,1:T(8,128)}), f32[1024,104]{0,1:T(8,128)}) %all-reduce.9.cloned.1.call-update) | async-done | bytes 426000 | tf_op jit(solution)/shard_map/psum | solution.py:346
  154.1 5.2 fusion.55
  159.3 15.2 %scan_forward.1 = (f32[1024,288]{1,0:T(8,128)}, f32[8,16,288]{2,1,0:T(8,128)}) custom-call(f32[1024,288]{1,0:T(8,128)} %get-tuple-element.121.step_ref, f32[1024,288]{1,0:T(8,128)} %get-tuple-element.120.drive_ref, f32[64,32,16]{2,1,0:T(8,128)} %bitcast.113, f32[16,288]{1,0:T(8,128)} %bitcast_multiply_fusion.1.a_ref), custom_call_target="tpu_custom_call" | custom-call | flops 37748736 | bytes 3538944 | tf_op jit(solution)/shard_map/scan_forward/pallas_call | solution.py:176
  174.5 6.0 multiply_convert_fusion.2
  185.3 41.6 %reduce-scatter.10.cloned.1.call-done = bf16[128,1152]{1,0:T(8,128)(2,1)} async-done(((bf16[1024,1152]{1,0:T(8,128)(2,1)}), bf16[128,1152]{1,0:T(8,128)(2,1)}) %reduce-scatter.10.cloned.1.call-update) | async-done | bytes 294928 | tf_op jit(solution)/shard_map/reduce_scatter | solution.py:357
  229.4 15.5 %all_to_all.15 = bf16[4,40,1152]{2,1,0:T(8,128)(2,1)} all-to-all(bf16[4,40,1152]{2,1,0:T(8,128)(2,1)S(1)} %bitcast.111), channel_id=1, replica_groups=mesh['exp'=4,'hid'=8] {'exp'}, dimensions={0} | all-to-all | bytes 737280 | tf_op jit(solution)/shard_map/all_to_all | solution.py:376
  245.4 13.4 %all_to_all.16 = bf16[4,40,1152]{2,1,0:T(8,128)(2,1)} all-to-all(bf16[4,40,1152]{2,1,0:T(8,128)(2,1)S(1)} %bitcast.112), channel_id=1, replica_groups=mesh['exp'=4,'hid'=8] {'exp'}, dimensions={0} | all-to-all | bytes 737280 | tf_op jit(solution)/shard_map/all_to_all | solution.py:376
  259.0 15.6 %all-gather.11.cloned.1.call-done = bf16[1280,1152]{1,0:T(8,128)(2,1)} async-done(((bf16[160,1152]{1,0:T(8,128)(2,1)}), bf16[1280,1152]{1,0:T(8,128)(2,1)}) %all-gather.11.cloned.1.call-update) | async-done | bytes 2949136 | tf_op jit(solution)/shard_map/all_gather | solution.py:378
  274.6 9.5 %fusion.4 = (bf16[1280,384]{1,0:T(8,128)(2,1)}, f32[1280,384]{1,0:T(8,128)}) fusion(bf16[1280,1152]{1,0:T(8,128)(2,1)} %all-gather.11.cloned.1.call-done, bf16[1,1152,384]{2,1,0:T(8,128)(2,1)S(1)} %copy-done), kind=kOutput, calls=%fused_computation.19 | convolution fusion | flops 1164410880 | bytes 6782976 | tf_op jit(solution)/shard_map/dot_general | solution.py:35
  284.1 23.7 %all-gather.13.cloned.1.call-done = bf16[1280,1152]{1,0:T(8,128)(2,1)} async-done(((bf16[160,1152]{1,0:T(8,128)(2,1)}), bf16[1280,1152]{1,0:T(8,128)(2,1)}) %all-gather.13.cloned.1.call-update) | async-done | bytes 2949136 | tf_op jit(solution)/shard_map/all_gather | solution.py:378
  319.2 8.9 %copy.150 = bf16[1280,2304]{1,0:T(8,128)(2,1)} copy(bf16[1280,2304]{0,1:T(8,128)(2,1)} %pad_maximum_fusion) | data formatting | bytes 11796480
  328.2 59.7 %reduce-scatter.16.cloned.1.call-done = bf16[160,2304]{1,0:T(8,128)(2,1)} async-done(((bf16[1280,2304]{1,0:T(8,128)(2,1)}), bf16[160,2304]{1,0:T(8,128)(2,1)}) %reduce-scatter.16.cloned.1.call-update) | async-done | bytes 737296 | tf_op jit(solution)/shard_map/reduce_scatter | solution.py:389
  387.9 23.6 %all_to_all.17 = bf16[4,40,2304]{2,1,0:T(8,128)(2,1)S(1)} all-to-all(bf16[4,40,2304]{2,1,0:T(8,128)(2,1)} %bitcast.115), channel_id=1, replica_groups=mesh['exp'=4,'hid'=8] {'exp'}, dimensions={0} | all-to-all | bytes 1474560 | tf_op jit(solution)/shard_map/all_to_all | solution.py:397
  414.1 26.9 %all-gather.15.cloned.1.call-done = bf16[1024,1152]{1,0:T(8,128)(2,1)} async-done(((bf16[128,1152]{1,0:T(8,128)(2,1)}), bf16[1024,1152]{1,0:T(8,128)(2,1)}) %all-gather.15.cloned.1.call-update) | async-done | bytes 2359312 | tf_op jit(solution)/shard_map/all_gather | solution.py:412
  441.1 6.9 multiply_reduce_fusion
  448.0 37.3 %scan_backward.1 = (f32[1024,288]{1,0:T(8,128)}, f32[1024,288]{1,0:T(8,128)}, f32[8,8,2048]{2,1,0:T(8,128)}, f32[8,8,2048]{2,1,0:T(8,128)}, f32[16,288]{1,0:T(8,128)}) custom-call(f32[1024,288]{1,0:T(8,128)} %get-tuple-element.121.step_ref, f32[1024,288]{1,0:T(8,128)} %get-tuple-element.120.drive_ref, f32[1024,288]{1,0:T(8,128)} %get-tuple-element.111.grad_ref, ...), custom_call_target="tpu_custom_call" | custom-call | flops 113246208 | bytes 5898240 | tf_op jit(solution)/shard_map/scan_backward/pallas_call | solution.py:213
  498.0 28.2 %all-reduce.10 = bf16[1024,104]{0,1:T(8,128)(2,1)S(1)} all-reduce(f32[1024,104]{0,1:T(8,128)S(1)} %pad_maximum_fusion.2), channel_id=1, replica_groups=mesh['exp'=4,'hid'=8] {'hid'}, use_global_device_ids=true, to_apply=%region_8.9 | all-reduce | flops 106496 | bytes 638976 | tf_op jit(solution)/shard_map/psum | solution.py:428
  557.0 5.0 convolution_bitcast_fusion
  570.5 35.4 %reduce-scatter.18.cloned.1.call-done = f32[72,1408]{1,0:T(8,128)} async-done(((f32[288,1408]{1,0:T(8,128)}), f32[72,1408]{1,0:T(8,128)}) %reduce-scatter.18.cloned.1.call-update) | async-done | bytes 405520
  610.8 39.8 %reduce-scatter.12.cloned.1.call-done = bf16[128,1152]{1,0:T(8,128)(2,1)} async-done(((bf16[1024,1152]{1,0:T(8,128)(2,1)}), bf16[128,1152]{1,0:T(8,128)(2,1)}) %reduce-scatter.12.cloned.1.call-update) | async-done | bytes 294928 | tf_op jit(solution)/shard_map/reduce_scatter | solution.py:448
  651.8 39.5 %all-reduce.5 = (f32[1152]{0:T(1024)}, f32[1152]{0:T(1024)}) all-reduce(f32[1152]{0:T(1024)S(1)} %get-tuple-element.99, f32[1152]{0:T(1024)S(1)} %get-tuple-element.93), channel_id=1, replica_groups=mesh['exp'=4,'hid'=8] {'exp','hid'}, use_global_device_ids=true, to_apply=%region_12.13 | all-reduce | flops 2304 | bytes 18432 | tf_op jit(solution)/shard_map/psum | solution.py:484
  (210 shorter events, 110.9 us)
Async XLA Ops:
  7.2 267.4 %copy-start = (bf16[1,1152,384]{2,1,0:T(8,128)(2,1)S(1)}, bf16[1,1152,384]{2,1,0:T(8,128)(2,1)}, u32[]{:S(2)}) copy-start(bf16[1,1152,384]{2,1,0:T(8,128)(2,1)} %param.32) | copy-start | bytes 2654212
  7.3 52.9 %all-gather.9.cloned.1.call-start = ((), (), s32[]{:S(2)}) async-start(), calls=%async_computation.9 | async-start | bytes 1658880 | tf_op jit(solution)/shard_map/all_gather | solution.py:309
  8.0 81.8 %all-gather.7.cloned.1.call-start = ((), (), s32[]{:S(2)}) async-start(), calls=%async_computation.8 | async-start | bytes 2654208 | tf_op jit(solution)/shard_map/all_gather | solution.py:329
  11.7 140.0 %all-reduce.9.cloned.1.call-start = ((), (), s32[]{:S(2)}) async-start(), calls=%async_computation.10 | async-start | bytes 851968 | tf_op jit(solution)/shard_map/psum | solution.py:346
  14.0 13.7 %collective-permute-start = (bf16[72,1408]{1,0:T(8,128)(2,1)S(1)}, bf16[72,1408]{1,0:T(8,128)(2,1)S(1)}, u32[]{:S(2)}, u32[]{:S(2)}) collective-permute-start(bf16[72,1408]{1,0:T(8,128)(2,1)S(1)} %concatenate.30), channel_id=1, source_target_pairs={{0,0},{1,8},{2,1},{3,9},{4,2},{5,10},{6,3},{7,11},{8,4},{9,12},{10... | collective-permute-start | bytes 608264 | tf_op jit(solution)/shard_map/ppermute | solution.py:308
  59.6 114.9 %copy-start.33 = (f32[288]{0:T(512)}, f32[288]{0:T(512)S(1)}, u32[]{:S(2)}) copy-start(f32[288]{0:T(512)S(1)} %get-tuple-element.96) | copy-start | bytes 3460
  97.7 129.2 %reduce-scatter.10.cloned.1.call-start = ((), (), s32[]{:S(2)}) async-start(), calls=%async_computation.11 | async-start | bytes 2654208 | tf_op jit(solution)/shard_map/reduce_scatter | solution.py:357
  184.2 42.7 %copy-start.2 = (bf16[1,128,1152]{2,1,0:T(8,128)(2,1)S(1)}, bf16[1,128,1152]{2,1,0:T(8,128)(2,1)}, u32[]{:S(2)}) copy-start(bf16[1,128,1152]{2,1,0:T(8,128)(2,1)} %param.17) | copy-start | bytes 884740
  184.2 60.7 %copy-start.11 = (bf16[1,128,1152]{2,1,0:T(8,128)(2,1)S(1)}, bf16[1,128,1152]{2,1,0:T(8,128)(2,1)}, u32[]{:S(2)}) copy-start(bf16[1,128,1152]{2,1,0:T(8,128)(2,1)} %param.20) | copy-start | bytes 884740
  184.3 90.3 %all-gather.11.cloned.1.call-start = ((), (), s32[]{:S(2)}) async-start(), calls=%async_computation.12 | async-start | bytes 3317760 | tf_op jit(solution)/shard_map/all_gather | solution.py:378
  228.1 184.1 %copy-start.27 = (f32[128]{0:T(128)}, f32[128]{0:T(128)S(1)}, u32[]{:S(2)}) copy-start(f32[128]{0:T(128)S(1)} %fusion.80) | copy-start | bytes 1540
  244.9 62.8 %all-gather.13.cloned.1.call-start = ((), (), s32[]{:S(2)}) async-start(), calls=%async_computation.13 | async-start | bytes 3317760 | tf_op jit(solution)/shard_map/all_gather | solution.py:378
  258.8 129.1 %reduce-scatter.16.cloned.1.call-start = ((), (), s32[]{:S(2)}) async-start(), calls=%async_computation.17 | async-start | bytes 6635520 | tf_op jit(solution)/shard_map/reduce_scatter | solution.py:389
  328.1 112.9 %all-gather.15.cloned.1.call-start = ((), (), s32[]{:S(2)}) async-start(), calls=%async_computation.14 | async-start | bytes 2654208 | tf_op jit(solution)/shard_map/all_gather | solution.py:412
  413.9 154.8 %reduce-scatter.14.cloned.1.call-start = ((), (), s32[]{:S(2)}) async-start(), calls=%async_computation.16 | async-start | bytes 1658880 | tf_op jit(solution)/shard_map/reduce_scatter | solution.py:469
  536.5 69.4 %reduce-scatter.18.cloned.1.call-start = ((), (), s32[]{:S(2)}) async-start(), calls=%async_computation.18 | async-start | bytes 2027520
  551.1 99.4 %reduce-scatter.12.cloned.1.call-start = ((), (), s32[]{:S(2)}) async-start(), calls=%async_computation.15 | async-start | bytes 2654208 | tf_op jit(solution)/shard_map/reduce_scatter | solution.py:448
  562.0 88.5 %copy-start.30 = (f32[128]{0:T(128)S(1)}, f32[128]{0:T(128)}, u32[]{:S(2)}) copy-start(f32[128]{0:T(128)} %copy-done.29) | copy-start | bytes 1540
  565.0 86.8 %copy-start.39 = (f32[128]{0:T(128)S(1)}, f32[128]{0:T(128)}, u32[]{:S(2)}) copy-start(f32[128]{0:T(128)} %copy-done.38) | copy-start | bytes 1540
  565.0 126.3 %copy-start.4 = (f32[128,2304]{1,0:T(8,128)S(1)}, f32[128,2304]{1,0:T(8,128)}, u32[]{:S(2)}) copy-start(f32[128,2304]{1,0:T(8,128)} %copy-done.3) | copy-start | bytes 3538948
  565.0 126.3 %copy-start.28 = (f32[128]{0:T(128)S(1)}, f32[128]{0:T(128)}, u32[]{:S(2)}) copy-start(f32[128]{0:T(128)} %copy-done.27) | copy-start | bytes 1540
  565.0 126.3 %copy-start.37 = (f32[128]{0:T(128)S(1)}, f32[128]{0:T(128)}, u32[]{:S(2)}) copy-start(f32[128]{0:T(128)} %copy-done.36) | copy-start | bytes 1540
  605.9 87.6 %collective-permute-start.1 = (f32[72,1408]{1,0:T(8,128)}, f32[72,1408]{1,0:T(8,128)}, u32[]{:S(2)}, u32[]{:S(2)}) collective-permute-start(f32[72,1408]{1,0:T(8,128)} %reduce-scatter.18.cloned.1.call-done), channel_id=1, source_target_pairs={{0,0},{8,1},{1,2},{9,3},{2,4},{10,5},{3,6},{11,7},{4,8},{12,9},{5,... | collective-permute-start | bytes 1216520 | tf_op jit(solution)/shard_map/ppermute | solution.py:478
  651.8 51.2 %copy-start.1 = (bf16[1,1152,384]{2,1,0:T(8,128)(2,1)S(1)}, bf16[1,1152,384]{2,1,0:T(8,128)(2,1)}, u32[]{:S(2)}) copy-start(bf16[1,1152,384]{2,1,0:T(8,128)(2,1)} %param.32) | copy-start | bytes 2654212
  (37 other events, 231.5 us)
Sparse Core Ops, SparseCore 0:
  9.6 48.7 all-gather.8
  60.9 28.8 all-gather.6
  97.8 53.7 all-reduce.8
  184.4 42.4 reduce-scatter.9
  245.1 29.4 all-gather.10
  276.3 31.3 all-gather.12
  328.2 59.6 reduce-scatter.15
  414.0 26.9 all-gather.14
  536.7 31.9 reduce-scatter.13
  570.8 35.0 reduce-scatter.17
  609.3 41.2 reduce-scatter.11
